TPU v7x, 32 devices: a whole 2x2x4 slice. The times are simulated.
32 devices in a mesh: ord: 8 (over z, y), blk: 4 (over x, core).
Axes of the slice: x: 2, y: 2, z: 4, core: 2. Of those that a mesh axis runs over, the one named last changes fastest.
Arguments:
- panel: bfloat16 [2880, 64, 2880], P('ord', 'blk'), as said below
- gauss: bfloat16 [2, 16, 2880, 2880], P(None, None, 'ord', 'blk'), may hold values from -2.3841858e-06 to 2.3841858e-06
- height: float32 [16], replicated, may hold values from 0.25 to 2.5
- order_map: int32 [2880], replicated, may hold values from 0 to 2879, as said below
- cycle_map: int32 [64], P('blk'), may hold values from 360 to 2519, as said below
Outputs:
- field: bfloat16 [5760, 3072], P('ord', 'blk')
Inputs may be any that keep to these rules, and one draw needn't show every extreme that they name: `order_map`: a permutation of 0 to 2879; the 360 slots of each index of ord hold consecutive orders in ascending order. `panel`: entries at degrees below the order of their slot are zero. `cycle_map`: distinct cycle numbers.
All inputs are finite; a program needn't handle non-finite values.
Results may differ from a plain program's by a relative error of at most 0.0068.
Values may be sent and summed in bfloat16 or wider, within the bound.
A program may use at most 256 MiB of HBM per device.

v0:
```python
import math

import jax
import jax.numpy as jnp
from jax import lax
from jax.sharding import PartitionSpec as P

ORDERS = 2880
TILE = 320
NLON = 5760


def cycle_angles(cycle_map):
    theta = math.pi * (cycle_map.astype(jnp.float32) + 0.5) / ORDERS
    return (jnp.cos(theta), jnp.sin(theta))


def legendre_tables(current, before, degree, orders, cosine, sine):
    deg = degree[None, None, :]
    order = orders[:, None, None]
    radial = (deg + 1.0) * current
    polar = (
        -(
            deg * cosine[None, :, None] * current
            - jnp.sqrt(jnp.maximum(deg * deg - order * order, 0.0)) * before
        )
        / sine[None, :, None]
    )
    azimuth = order * current / sine[None, :, None]
    return jnp.stack([radial, polar, azimuth], 2).astype(jnp.bfloat16)


def weighted(coef, degree, height):
    radial = jnp.exp(-(degree[None, :] + 2.0) * height[:, None] / ORDERS)
    return (coef.astype(jnp.float32) * radial[None, :, None, :]).astype(jnp.bfloat16)


def assemble(total, cycles, shells):
    count = total.shape[1]
    parts = total.reshape(2, count, cycles, 3, shells)
    g_part = parts[0]
    h_part = parts[1]
    cosine_part = jnp.concatenate([g_part[:, :, :2], -h_part[:, :, 2:]], 2)
    sine_part = jnp.concatenate([h_part[:, :, :2], g_part[:, :, 2:]], 2)
    return (
        jnp.stack([cosine_part, sine_part])
        .reshape(2, count, cycles * 3 * shells)
        .astype(jnp.bfloat16)
    )


def phase_angles(orders_int, position):
    phase = orders_int[:, None] * position[None, :] % NLON
    angle = phase.astype(jnp.float32) * (2.0 * math.pi / NLON)
    return (jnp.cos(angle), jnp.sin(angle))


def degree_sums(panel_src, edge, coef_src, orders, cosine, sine, height, base, first, last):
    count, cycles, _ = panel_src.shape
    shells = height.shape[0]

    def step(tile, total):
        offset = (tile * TILE - base).astype(jnp.int32)
        current = lax.dynamic_slice_in_dim(panel_src, offset, TILE, 2).astype(jnp.float32)
        earlier = lax.dynamic_slice_in_dim(panel_src, jnp.maximum(offset - 1, 0), TILE, 2).astype(
            jnp.float32
        )
        shifted = jnp.concatenate([edge[:, :, None].astype(jnp.float32), current[:, :, :-1]], 2)
        before = jnp.where(offset > 0, earlier, shifted)
        degree = (tile * TILE + jnp.arange(TILE)).astype(jnp.float32)
        tables = legendre_tables(current, before, degree, orders, cosine, sine).reshape(
            count, cycles * 3, TILE
        )
        weights = weighted(lax.dynamic_slice_in_dim(coef_src, offset, TILE, 3), degree, height)
        return total + jnp.einsum(
            "okl,gsol->goks", tables, weights, preferred_element_type=jnp.float32
        )

    init = jnp.zeros((2, count, cycles * 3, shells), jnp.float32)
    return lax.fori_loop(jnp.asarray(first, jnp.int32), jnp.asarray(last, jnp.int32), step, init)


def body(panel, gauss, height, order_map, cycle_map):
    count, cycles, degrees = panel.shape
    shells = height.shape[0]
    tiles = degrees // TILE
    cosine, sine = cycle_angles(cycle_map)
    coef = lax.all_gather(gauss, "blk", axis=3, tiled=True)
    here = lax.axis_index("ord")
    orders_int = lax.dynamic_slice_in_dim(order_map, here * count, count, 0)
    orders = orders_int.astype(jnp.float32)
    zero_edge = jnp.zeros((count, cycles), jnp.bfloat16)
    total = degree_sums(panel, zero_edge, coef, orders, cosine, sine, height, 0, 0, tiles)
    spectra = assemble(total, cycles, shells)
    spread = lax.all_to_all(spectra, "ord", split_axis=2, concat_axis=1, tiled=True)
    items = spread.shape[2]
    width = NLON // 8
    inner_cos, inner_sin = phase_angles(order_map, jnp.arange(width))
    start_cos, start_sin = phase_angles(order_map, jnp.arange(8) * width)

    def transform(block):
        block_cos = lax.dynamic_slice_in_dim(start_cos, block, 1, 1)
        block_sin = lax.dynamic_slice_in_dim(start_sin, block, 1, 1)
        table_cos = inner_cos * block_cos - inner_sin * block_sin
        table_sin = inner_sin * block_cos + inner_cos * block_sin
        tables = jnp.stack([table_cos, table_sin]).astype(jnp.bfloat16)
        return lax.dot_general(
            tables, spread, (((0, 1), (0, 1)), ((), ())), preferred_element_type=jnp.float32
        )

    field = lax.map(transform, jnp.arange(8)).reshape(NLON, items).astype(jnp.bfloat16)
    return lax.all_to_all(field, "ord", split_axis=0, concat_axis=1, tiled=True)


def solution(mesh):
    return jax.shard_map(
        body,
        mesh=mesh,
        in_specs=(P("ord", "blk", None), P(None, None, "ord", "blk"), P(), P(), P("blk")),
        out_specs=P("ord", "blk"),
        check_vma=False,
    )
```

profile of v0, /device:TPU:0, one launch (start us, length us, event | category | flops | bytes accessed | tf_op | source)
XLA Modules:
  0.0 1558.1 jit_solution(583133086494186010)
XLA Ops:
  6.5 24.1 %copy.29 = bf16[2,16,360,720]{2,1,0,3:T(8,128)(2,1)} copy(bf16[2,16,360,720]{3,2,1,0:T(8,128)(2,1)} %param.10) | data formatting | bytes 33177600 | tf_op args[1]
  31.5 49.6 %copy.31 = bf16[360,16,2880]{0,2,1:T(8,128)(2,1)} copy(bf16[360,16,2880]{2,1,0:T(8,128)(2,1)} %param.9) | data formatting | bytes 66355200
  81.1 367.9 %all-gather.2.cloned.1.call-done = bf16[2,16,360,2880]{2,1,0,3:T(8,128)(2,1)} async-done(((bf16[2,16,360,720]{2,1,0,3:T(8,128)(2,1)}), bf16[2,16,360,2880]{2,1,0,3:T(8,128)(2,1)}) %all-gather.2.cloned.1.call-update) | async-done | bytes 66355216 | tf_op jit(solution)/shard_map/all_gather | solution.py:88
  449.0 670.7 %while.25 = (s32[]{:T(128)}, f32[2,360,48,16]{2,3,0,1:T(8,128)}, bf16[2,16,360,2880]{2,1,0,3:T(8,128)(2,1)}, f32[16]{0:T(128)S(1)}, bf16[360,16,2880]{0,2,1:T(8,...) while((s32[]{:T(128)}, f32[2,360,48,16]{2,3,0,1:T(8,128)}, ...), condition=%wide.region_1.2_spmd.clone, body=%wide.region_0.1_spmd.clone.sunk | while | flops 405015680 | bytes 134444624 | solution.py:80
  455.4 9.5 fusion.55
  464.9 6.1 pad_maximum_fusion.5
  471.0 18.0 %copy.44 = bf16[360,48,320,1]{2,1,3,0:T(8,128)(2,1)} copy(bf16[360,48,320,1]{0,2,1,3:T(8,128)(2,1)} %bitcast.76) | data formatting | bytes 22118400 | tf_op jit(solution)/shard_map/while/body/convert_element_type | solution.py:30
  489.0 7.1 constant_dynamic-slice_fusion.2
  496.1 13.6 copy.45
  509.7 11.4 bitcast_add_fusion.2
  527.5 9.5 fusion.55
  537.0 6.1 pad_maximum_fusion.5
  543.1 18.0 %copy.44 = bf16[360,48,320,1]{2,1,3,0:T(8,128)(2,1)} copy(bf16[360,48,320,1]{0,2,1,3:T(8,128)(2,1)} %bitcast.76) | data formatting | bytes 22118400 | tf_op jit(solution)/shard_map/while/body/convert_element_type | solution.py:30
  561.1 7.1 constant_dynamic-slice_fusion.2
  568.2 13.6 copy.45
  581.8 14.1 bitcast_add_fusion.2
  602.3 9.5 fusion.55
  611.8 6.1 pad_maximum_fusion.5
  617.9 18.0 %copy.44 = bf16[360,48,320,1]{2,1,3,0:T(8,128)(2,1)} copy(bf16[360,48,320,1]{0,2,1,3:T(8,128)(2,1)} %bitcast.76) | data formatting | bytes 22118400 | tf_op jit(solution)/shard_map/while/body/convert_element_type | solution.py:30
  635.9 7.1 constant_dynamic-slice_fusion.2
  643.0 13.6 copy.45
  656.6 14.1 bitcast_add_fusion.2
  677.1 9.5 fusion.55
  686.6 6.1 pad_maximum_fusion.5
  692.7 18.0 %copy.44 = bf16[360,48,320,1]{2,1,3,0:T(8,128)(2,1)} copy(bf16[360,48,320,1]{0,2,1,3:T(8,128)(2,1)} %bitcast.76) | data formatting | bytes 22118400 | tf_op jit(solution)/shard_map/while/body/convert_element_type | solution.py:30
  710.7 7.1 constant_dynamic-slice_fusion.2
  717.8 13.6 copy.45
  731.4 14.1 bitcast_add_fusion.2
  751.9 9.5 fusion.55
  767.5 18.0 %copy.44 = bf16[360,48,320,1]{2,1,3,0:T(8,128)(2,1)} copy(bf16[360,48,320,1]{0,2,1,3:T(8,128)(2,1)} %bitcast.76) | data formatting | bytes 22118400 | tf_op jit(solution)/shard_map/while/body/convert_element_type | solution.py:30
  785.5 7.1 constant_dynamic-slice_fusion.2
  792.6 13.6 copy.45
  806.2 14.1 bitcast_add_fusion.2
  826.7 9.5 fusion.55
  842.4 18.0 %copy.44 = bf16[360,48,320,1]{2,1,3,0:T(8,128)(2,1)} copy(bf16[360,48,320,1]{0,2,1,3:T(8,128)(2,1)} %bitcast.76) | data formatting | bytes 22118400 | tf_op jit(solution)/shard_map/while/body/convert_element_type | solution.py:30
  860.3 7.1 constant_dynamic-slice_fusion.2
  867.5 13.6 copy.45
  881.1 14.1 bitcast_add_fusion.2
  901.6 9.5 fusion.55
  917.2 18.0 %copy.44 = bf16[360,48,320,1]{2,1,3,0:T(8,128)(2,1)} copy(bf16[360,48,320,1]{0,2,1,3:T(8,128)(2,1)} %bitcast.76) | data formatting | bytes 22118400 | tf_op jit(solution)/shard_map/while/body/convert_element_type | solution.py:30
  935.2 7.1 constant_dynamic-slice_fusion.2
  942.3 13.6 copy.45
  955.9 14.1 bitcast_add_fusion.2
  976.4 9.6 fusion.55
  992.1 18.0 %copy.44 = bf16[360,48,320,1]{2,1,3,0:T(8,128)(2,1)} copy(bf16[360,48,320,1]{0,2,1,3:T(8,128)(2,1)} %bitcast.76) | data formatting | bytes 22118400 | tf_op jit(solution)/shard_map/while/body/convert_element_type | solution.py:30
  1010.1 7.1 constant_dynamic-slice_fusion.2
  1017.2 13.6 copy.45
  1030.8 14.1 bitcast_add_fusion.2
  1051.3 9.5 fusion.55
  1066.9 18.0 %copy.44 = bf16[360,48,320,1]{2,1,3,0:T(8,128)(2,1)} copy(bf16[360,48,320,1]{0,2,1,3:T(8,128)(2,1)} %bitcast.76) | data formatting | bytes 22118400 | tf_op jit(solution)/shard_map/while/body/convert_element_type | solution.py:30
  1084.9 7.1 constant_dynamic-slice_fusion.2
  1092.0 13.6 copy.45
  1105.6 14.1 bitcast_add_fusion.2
  1135.3 27.8 %all-to-all-done = bf16[2,360,768]{1,0,2:T(2,128)(2,1)S(1)} async-done(((bf16[2,360,768]{1,0,2:T(2,128)(2,1)}), bf16[2,360,768]{1,0,2:T(2,128)(2,1)S(1)}, u32[]{:S(2)}, u32[]{:S(2)}) %all-to-all-start) | async-done | bytes 1105952 | tf_op jit(solution)/shard_map/all_to_all | solution.py:95
  1164.7 352.7 %while.26 = (s32[]{:T(128)}, bf16[8,720,96]{1,2,0:T(8,128)(2,1)S(1)}, s32[8]{0:T(128)S(1)}, f32[2880,8]{0,1:T(8,128)}, f32[2880,8]{0,1:T(8,128)}, /*index=5*/bf1...) while((s32[]{:T(128)}, ...), condition=%wide.region_3.4_spmd.clone.clone, body=%wide.region_2.3_spmd.clone.clone.sunk | while | flops 835660800 | bytes 18279324 | solution.py:111
  1168.2 37.8 %fusion.58 = (bf16[1,2880,720]{1,2,0:T(8,128)(2,1)S(1)}, bf16[1,2880,720]{1,2,0:T(8,128)(2,1)S(1)}) fusion(s32[2880]{0:T(1024)S(1)} %get-tuple-element.493, f32[2880]{0:T(1024)S(1)} %get-tuple-element.418, f32[2880]{0:T(1024)S(1)} %get-tuple-element.419), kind=kLoop, calls=%fused_computation.32.clone.1 | loop fusion | flops 35251200 | bytes 8328960 | tf_op jit(solution)/shard_map/convert
  1212.3 37.8 %fusion.58 = (bf16[1,2880,720]{1,2,0:T(8,128)(2,1)S(1)}, bf16[1,2880,720]{1,2,0:T(8,128)(2,1)S(1)}) fusion(s32[2880]{0:T(1024)S(1)} %get-tuple-element.493, f32[2880]{0:T(1024)S(1)} %get-tuple-element.418, f32[2880]{0:T(1024)S(1)} %get-tuple-element.419), kind=kLoop, calls=%fused_computation.32.clone.1 | loop fusion | flops 35251200 | bytes 8328960 | tf_op jit(solution)/shard_map/convert
  1256.4 37.8 %fusion.58 = (bf16[1,2880,720]{1,2,0:T(8,128)(2,1)S(1)}, bf16[1,2880,720]{1,2,0:T(8,128)(2,1)S(1)}) fusion(s32[2880]{0:T(1024)S(1)} %get-tuple-element.493, f32[2880]{0:T(1024)S(1)} %get-tuple-element.418, f32[2880]{0:T(1024)S(1)} %get-tuple-element.419), kind=kLoop, calls=%fused_computation.32.clone.1 | loop fusion | flops 35251200 | bytes 8328960 | tf_op jit(solution)/shard_map/convert
  1300.5 37.8 %fusion.58 = (bf16[1,2880,720]{1,2,0:T(8,128)(2,1)S(1)}, bf16[1,2880,720]{1,2,0:T(8,128)(2,1)S(1)}) fusion(s32[2880]{0:T(1024)S(1)} %get-tuple-element.493, f32[2880]{0:T(1024)S(1)} %get-tuple-element.418, f32[2880]{0:T(1024)S(1)} %get-tuple-element.419), kind=kLoop, calls=%fused_computation.32.clone.1 | loop fusion | flops 35251200 | bytes 8328960 | tf_op jit(solution)/shard_map/convert
  1344.6 37.8 %fusion.58 = (bf16[1,2880,720]{1,2,0:T(8,128)(2,1)S(1)}, bf16[1,2880,720]{1,2,0:T(8,128)(2,1)S(1)}) fusion(s32[2880]{0:T(1024)S(1)} %get-tuple-element.493, f32[2880]{0:T(1024)S(1)} %get-tuple-element.418, f32[2880]{0:T(1024)S(1)} %get-tuple-element.419), kind=kLoop, calls=%fused_computation.32.clone.1 | loop fusion | flops 35251200 | bytes 8328960 | tf_op jit(solution)/shard_map/convert
  1388.7 37.8 %fusion.58 = (bf16[1,2880,720]{1,2,0:T(8,128)(2,1)S(1)}, bf16[1,2880,720]{1,2,0:T(8,128)(2,1)S(1)}) fusion(s32[2880]{0:T(1024)S(1)} %get-tuple-element.493, f32[2880]{0:T(1024)S(1)} %get-tuple-element.418, f32[2880]{0:T(1024)S(1)} %get-tuple-element.419), kind=kLoop, calls=%fused_computation.32.clone.1 | loop fusion | flops 35251200 | bytes 8328960 | tf_op jit(solution)/shard_map/convert
  1432.8 37.8 %fusion.58 = (bf16[1,2880,720]{1,2,0:T(8,128)(2,1)S(1)}, bf16[1,2880,720]{1,2,0:T(8,128)(2,1)S(1)}) fusion(s32[2880]{0:T(1024)S(1)} %get-tuple-element.493, f32[2880]{0:T(1024)S(1)} %get-tuple-element.418, f32[2880]{0:T(1024)S(1)} %get-tuple-element.419), kind=kLoop, calls=%fused_computation.32.clone.1 | loop fusion | flops 35251200 | bytes 8328960 | tf_op jit(solution)/shard_map/convert
  1476.9 37.8 %fusion.58 = (bf16[1,2880,720]{1,2,0:T(8,128)(2,1)S(1)}, bf16[1,2880,720]{1,2,0:T(8,128)(2,1)S(1)}) fusion(s32[2880]{0:T(1024)S(1)} %get-tuple-element.493, f32[2880]{0:T(1024)S(1)} %get-tuple-element.418, f32[2880]{0:T(1024)S(1)} %get-tuple-element.419), kind=kLoop, calls=%fused_computation.32.clone.1 | loop fusion | flops 35251200 | bytes 8328960 | tf_op jit(solution)/shard_map/convert
  1517.4 32.5 %all_to_all.34 = bf16[8,720,96]{1,2,0:T(8,128)(2,1)S(1)} all-to-all(bf16[8,720,96]{1,2,0:T(8,128)(2,1)S(1)} %get-tuple-element.155), channel_id=1, replica_groups=mesh['ord'=8,'blk'=4] {'ord'}, dimensions={0} | all-to-all | bytes 2211840 | tf_op jit(solution)/shard_map/all_to_all | solution.py:112
  (124 shorter events, 141.6 us)
Async XLA Ops:
  6.5 442.5 %all-gather.2.cloned.1.call-start = ((), (), s32[]{:S(2)}) async-start(), calls=%async_computation.2 | async-start | bytes 88473600 | tf_op jit(solution)/shard_map/all_gather | solution.py:88
  31.4 49.6 %copy-start.2 = (s32[16]{0:T(128)S(1)}, s32[16]{0:T(128)}, u32[]{:S(2)}) copy-start(s32[16]{0:T(128)} %param.13) | copy-start | bytes 196
  31.5 417.6 %copy-start.1 = (f32[16]{0:T(128)S(1)}, f32[16]{0:T(128)}, u32[]{:S(2)}) copy-start(f32[16]{0:T(128)} %param.11) | copy-start | bytes 196
  1125.6 8.6 copy-start
  1128.6 34.5 %all-to-all-start = ((bf16[2,360,768]{1,0,2:T(2,128)(2,1)}), bf16[2,360,768]{1,0,2:T(2,128)(2,1)S(1)}, u32[]{:S(2)}, u32[]{:S(2)}) async-start(bf16[2,360,768]{1,0,2:T(2,128)(2,1)} %copy.34), calls=%async_computation | async-start | bytes 2359296 | tf_op jit(solution)/shard_map/all_to_all | solution.py:95
Sparse Core Ops, SparseCore 0:
  30.8 418.2 all-gather.1
where the time goes:
time: 1570 us; the launch traced here: 1560 us
  other arithmetic  503 us (32%)
  local copies, waits for them, and re-layouts  446 us (28%)
  waiting for transfers between devices  396 us (25%)
  matrix products  146 us (9%)
  blocking collectives  32.5 us (2%)
    all_gather x1, waiting for transfers between devices, body(): coef = lax.all_gather(gauss, 'blk', axis=3, tiled=True)  368 us
    another operation x9, other arithmetic  303 us
    dynamic_slice x18, local copies, waits for them, and re-layouts, step(): lax.dynamic_slice_in_dim(coef_src, offset, TILE, 3)  186 us
    convert_element_type x9, local copies, waits for them, and re-layouts, legendre_tables(): return jnp.stack([radial, polar, azimuth], 2).astype(jnp.bfloat16)  162 us
    another operation x18, other arithmetic, legendre_tables(): return jnp.stack([radial, polar, azimuth], 2).astype(jnp.bfloat16)  141 us
    dot_general x9, matrix products, step(): jnp.einsum('okl,gsol->goks', tables, weights, preferred_element_type=jnp....  124 us
    unnamed x8, local copies, waits for them, and re-layouts  73.7 us
    convert_element_type x9, other arithmetic, step(): lax.dynamic_slice_in_dim(panel_src, offset, TILE, 2).astype(jnp.float32)  54.1 us
  transfers between devices with their start and end apart: 2, of which 2 were waited for; matrix products, arithmetic and copies ran while one was open for 3% of the time, Pallas kernels for 0%

commit v1 on v0

--- a/solution.py
+++ b/solution.py
@@ -8,6 +8,7 @@
 ORDERS = 2880
 TILE = 320
 NLON = 5760
+GROUPS = 3
 
 
 def cycle_angles(cycle_map):
@@ -49,10 +50,36 @@
     )
 
 
-def phase_angles(orders_int, position):
-    phase = orders_int[:, None] * position[None, :] % NLON
-    angle = phase.astype(jnp.float32) * (2.0 * math.pi / NLON)
+def turn(steps, period):
+    angle = (steps % period).astype(jnp.float32) * (2.0 * math.pi / period)
     return (jnp.cos(angle), jnp.sin(angle))
+
+
+def synthesis(spread, order_map, ranks):
+    items = spread.shape[2]
+    count = spread.shape[1] // ranks
+    period = NLON // count
+    rows = NLON // period
+    block = order_map.reshape(ranks, count)[:, 0] // count
+    p = jnp.arange(period, dtype=jnp.int32)
+    q = jnp.arange(rows, dtype=jnp.int32)
+    r = jnp.arange(count, dtype=jnp.int32)
+    block_cos, block_sin = turn(p[:, None] * block[None, :], period)
+    mix = jnp.stack(
+        [jnp.stack([block_cos, block_sin], 1), jnp.stack([-block_sin, block_cos], 1)], 1
+    )
+    parts = spread.reshape(2, ranks, count, items)
+    mixed = jnp.einsum(
+        "pckd,kdri->pcri", mix, parts.astype(jnp.float32), precision=lax.Precision.HIGHEST
+    ).astype(jnp.bfloat16)
+    p_cos, p_sin = turn(p[:, None] * r[None, :], NLON)
+    q_cos, q_sin = turn(r[:, None] * q[None, :] * period, NLON)
+    p_cos, p_sin = p_cos[:, :, None], p_sin[:, :, None]
+    tables = jnp.stack([p_cos * q_cos - p_sin * q_sin, p_sin * q_cos + p_cos * q_sin], 1)
+    field = jnp.einsum(
+        "pcrq,pcri->pqi", tables.astype(jnp.bfloat16), mixed, preferred_element_type=jnp.float32
+    )
+    return field.astype(jnp.bfloat16).transpose(1, 0, 2).reshape(NLON, items)
 
 
 def degree_sums(panel_src, edge, coef_src, orders, cosine, sine, height, base, first, last):
@@ -85,30 +112,25 @@
     shells = height.shape[0]
     tiles = degrees // TILE
     cosine, sine = cycle_angles(cycle_map)
-    coef = lax.all_gather(gauss, "blk", axis=3, tiled=True)
     here = lax.axis_index("ord")
     orders_int = lax.dynamic_slice_in_dim(order_map, here * count, count, 0)
     orders = orders_int.astype(jnp.float32)
-    zero_edge = jnp.zeros((count, cycles), jnp.bfloat16)
-    total = degree_sums(panel, zero_edge, coef, orders, cosine, sine, height, 0, 0, tiles)
+    groups = GROUPS if count % GROUPS == 0 else 1
+    size = count // groups
+    zero_edge = jnp.zeros((size, cycles), jnp.bfloat16)
+    totals = []
+    for group in range(groups):
+        part = slice(group * size, (group + 1) * size)
+        coef = lax.all_gather(gauss[:, :, part], "blk", axis=3, tiled=True)
+        totals.append(
+            degree_sums(
+                panel[part], zero_edge, coef, orders[part], cosine, sine, height, 0, 0, tiles
+            )
+        )
+    total = jnp.concatenate(totals, 1)
     spectra = assemble(total, cycles, shells)
     spread = lax.all_to_all(spectra, "ord", split_axis=2, concat_axis=1, tiled=True)
-    items = spread.shape[2]
-    width = NLON // 8
-    inner_cos, inner_sin = phase_angles(order_map, jnp.arange(width))
-    start_cos, start_sin = phase_angles(order_map, jnp.arange(8) * width)
-
-    def transform(block):
-        block_cos = lax.dynamic_slice_in_dim(start_cos, block, 1, 1)
-        block_sin = lax.dynamic_slice_in_dim(start_sin, block, 1, 1)
-        table_cos = inner_cos * block_cos - inner_sin * block_sin
-        table_sin = inner_sin * block_cos + inner_cos * block_sin
-        tables = jnp.stack([table_cos, table_sin]).astype(jnp.bfloat16)
-        return lax.dot_general(
-            tables, spread, (((0, 1), (0, 1)), ((), ())), preferred_element_type=jnp.float32
-        )
-
-    field = lax.map(transform, jnp.arange(8)).reshape(NLON, items).astype(jnp.bfloat16)
+    field = synthesis(spread, order_map, order_map.shape[0] // count)
     return lax.all_to_all(field, "ord", split_axis=0, concat_axis=1, tiled=True)
 
 

time: 1570 us -> 1060 us (0.68)
  waiting for transfers between devices: 396 us -> 76.9 us
  other arithmetic: 503 us -> 219 us
  local copies, waits for them, and re-layouts: 446 us -> 538 us
  matrix products: 146 us -> 166 us
    all_gather x1 -> x3, waiting for transfers between devices: 368 us -> 55.5 us  [body(): coef = lax.all_gather(gauss[:, :, part], 'blk', axis=3, tiled=True)]
    another operation x9 -> x3, other arithmetic: 303 us -> 5 us
    slice x0 -> x2, local copies, waits for them, and re-layouts: none -> 38 us  [the longest x1 24.6 us: body(): panel[part]]
    dynamic_slice x18 -> x54, local copies, waits for them, and re-layouts: 186 us -> 222 us  [step(): lax.dynamic_slice_in_dim(coef_src, offset, TILE, 3)]
    dot_general x9 -> x27, matrix products: 124 us -> 157 us  [step(): jnp.einsum('okl,gsol->goks', tables, weights, preferred_element_type=jnp....]
    convert_element_type x9 -> x27, local copies, waits for them, and re-layouts: 162 us -> 185 us  [legendre_tables(): return jnp.stack([radial, polar, azimuth], 2).astype(jnp.bfloat16)]
    another operation x18 -> x54, other arithmetic: 141 us -> 161 us  [legendre_tables(): return jnp.stack([radial, polar, azimuth], 2).astype(jnp.bfloat16)]
    convert_element_type x9 -> x27, other arithmetic: 54.1 us -> 42.4 us  [step(): lax.dynamic_slice_in_dim(panel_src, offset, TILE, 2).astype(jnp.float32)]
  transfers between devices with their start and end apart: 2 -> 4, of which waited for: 2 -> 2; matrix products, arithmetic and copies ran while one was open for 3% -> 59% of each run, Pallas kernels for 0% -> 0%
where the time goes in v1:
time: 1060 us; the launch traced here: 1050 us
  local copies, waits for them, and re-layouts  538 us (51%)
  other arithmetic  219 us (21%)
  matrix products  166 us (16%)
  waiting for transfers between devices  76.9 us (7%)
  blocking collectives  32.5 us (3%)
  between operations  13.3 us (1%)
    dynamic_slice x54, local copies, waits for them, and re-layouts, step(): lax.dynamic_slice_in_dim(coef_src, offset, TILE, 3)  222 us
    convert_element_type x27, local copies, waits for them, and re-layouts, legendre_tables(): return jnp.stack([radial, polar, azimuth], 2).astype(jnp.bfloat16)  185 us
    another operation x54, other arithmetic, legendre_tables(): return jnp.stack([radial, polar, azimuth], 2).astype(jnp.bfloat16)  161 us
    dot_general x27, matrix products, step(): jnp.einsum('okl,gsol->goks', tables, weights, preferred_element_type=jnp....  157 us
    unnamed x20, local copies, waits for them, and re-layouts  76.1 us
    all_gather x3, waiting for transfers between devices, body(): coef = lax.all_gather(gauss[:, :, part], 'blk', axis=3, tiled=True)  55.5 us
    convert_element_type x27, other arithmetic, step(): lax.dynamic_slice_in_dim(panel_src, offset, TILE, 2).astype(jnp.float32)  42.4 us
    all_to_all x1, blocking collectives, body(): return lax.all_to_all(field, 'ord', split_axis=0, concat_axis=1, tiled=True)  32.5 us
  transfers between devices with their start and end apart: 4, of which 2 were waited for; matrix products, arithmetic and copies ran while one was open for 59% of the time, Pallas kernels for 0%

profile of v1, /device:TPU:0, one launch (start us, length us, event | category | flops | bytes accessed | tf_op | source)
XLA Modules:
  0.0 1052.9 jit_solution(16602426517486135220)
XLA Ops:
  6.5 13.4 %fusion.70 = (bf16[2,16,120,720]{3,2,1,0:T(8,128)(2,1)}, bf16[2,16,120,720]{3,2,1,0:T(8,128)(2,1)}, bf16[2,16,120,720]{3,2,1,0:T(8,128)(2,1)}) fusion(bf16[2,16,360,720]{3,2,1,0:T(8,128)(2,1)} %param.12), kind=kLoop, calls=%fused_computation.131 | loop fusion | bytes 33177600 | tf_op jit(solution)/shard_map/slice | solution.py:124
  19.9 8.8 copy.101
  28.8 8.8 copy.102
  37.7 9.8 copy.103
  49.0 24.6 %fusion.69 = (bf16[120,16,2880]{2,1,0:T(8,128)(2,1)}, bf16[120,16,2880]{2,1,0:T(8,128)(2,1)}, bf16[120,16,2880]{2,1,0:T(8,128)(2,1)}) fusion(bf16[360,16,2880]{2,1,0:T(8,128)(2,1)} %param.11), kind=kLoop, calls=%fused_computation.130 | loop fusion | bytes 66355200 | tf_op jit(solution)/shard_map/slice | solution.py:127
  73.6 16.1 %copy.104 = bf16[120,16,2880]{0,2,1:T(8,128)(2,1)} copy(bf16[120,16,2880]{2,1,0:T(8,128)(2,1)} %get-tuple-element.521) | data formatting | bytes 22118400
  89.7 16.1 %copy.105 = bf16[120,16,2880]{0,2,1:T(8,128)(2,1)} copy(bf16[120,16,2880]{2,1,0:T(8,128)(2,1)} %get-tuple-element.522) | data formatting | bytes 22118400
  105.8 16.4 %copy.106 = bf16[120,16,2880]{0,2,1:T(8,128)(2,1)} copy(bf16[120,16,2880]{2,1,0:T(8,128)(2,1)} %get-tuple-element.523) | data formatting | bytes 22118400
  122.2 55.5 %all-gather.4.cloned.1.call-done = bf16[2,16,120,2880]{2,1,0,3:T(8,128)(2,1)} async-done(((bf16[2,16,120,720]{2,1,0,3:T(8,128)(2,1)}), bf16[2,16,120,2880]{2,1,0,3:T(8,128)(2,1)}) %all-gather.4.cloned.1.call-update) | async-done | bytes 22118416 | tf_op jit(solution)/shard_map/all_gather | solution.py:124
  177.7 261.1 %while.39 = (s32[]{:T(128)}, f32[2,120,48,16]{2,3,0,1:T(8,128)}, bf16[2,16,120,2880]{2,1,0,3:T(8,128)(2,1)}, f32[16]{0:T(128)S(1)}, bf16[120,16,2880]{0,2,1:T(8,...) while((s32[]{:T(128)}, f32[2,120,48,16]{2,3,0,1:T(8,128)}, ...), condition=%wide.region_1.2_spmd.clone, body=%wide.region_0.1_spmd.clone.sunk | while | flops 135017616 | bytes 44875640 | solution.py:107
  185.5 7.4 copy.123
  215.1 6.8 copy.123
  230.1 5.9 bitcast_add_fusion.6
  243.7 6.9 copy.123
  258.7 5.9 bitcast_add_fusion.6
  272.4 6.9 copy.123
  287.5 5.9 bitcast_add_fusion.6
  301.1 6.8 copy.123
  316.3 5.9 bitcast_add_fusion.6
  330.0 7.1 copy.123
  346.3 6.5 bitcast_add_fusion.6
  360.5 6.8 copy.123
  375.5 6.1 bitcast_add_fusion.6
  389.3 6.8 copy.123
  404.3 5.9 bitcast_add_fusion.6
  417.9 6.8 copy.123
  433.0 5.9 bitcast_add_fusion.6
  442.5 256.3 %while.40 = (s32[]{:T(128)}, f32[2,120,48,16]{2,3,0,1:T(8,128)}, bf16[2,16,120,2880]{2,1,0,3:T(8,128)(2,1)}, f32[16]{0:T(128)S(1)}, bf16[120,16,2880]{0,2,1:T(8,...) while((s32[]{:T(128)}, f32[2,120,48,16]{2,3,0,1:T(8,128)}, ...), condition=%wide.region_3.4_spmd.clone, body=%wide.region_2.3_spmd.clone.sunk | while | flops 135017616 | bytes 44875640 | solution.py:107
  450.3 6.8 copy.125
  478.1 6.8 copy.125
  493.0 5.9 bitcast_add_fusion.7
  506.6 6.8 copy.125
  521.6 5.9 bitcast_add_fusion.7
  535.2 6.8 copy.125
  550.1 5.9 bitcast_add_fusion.7
  563.7 6.8 copy.125
  578.7 5.9 bitcast_add_fusion.7
  592.4 6.8 copy.125
  607.3 5.9 bitcast_add_fusion.7
  620.9 6.8 copy.125
  635.8 5.9 bitcast_add_fusion.7
  649.4 6.8 copy.125
  664.3 5.9 bitcast_add_fusion.7
  677.9 6.8 copy.125
  692.9 5.9 bitcast_add_fusion.7
  702.4 257.9 %while.41 = (s32[]{:T(128)}, f32[2,120,48,16]{2,3,0,1:T(8,128)}, bf16[2,16,120,2880]{2,1,0,3:T(8,128)(2,1)}, f32[16]{0:T(128)S(1)}, bf16[120,16,2880]{0,2,1:T(8,...) while((s32[]{:T(128)}, f32[2,120,48,16]{2,3,0,1:T(8,128)}, ...), condition=%wide.region_5.6_spmd.clone, body=%wide.region_4.5_spmd.clone.sunk | while | flops 135017616 | bytes 44875640 | solution.py:107
  710.2 6.9 copy.127
  738.4 6.9 copy.127
  753.5 5.8 bitcast_add_fusion.8
  767.1 6.9 copy.127
  782.2 5.8 bitcast_add_fusion.8
  795.8 6.9 copy.127
  810.9 5.8 bitcast_add_fusion.8
  824.5 6.9 copy.127
  853.2 6.9 copy.127
  868.3 5.8 bitcast_add_fusion.8
  882.0 6.9 copy.127
  910.7 6.9 copy.127
  925.8 5.8 bitcast_add_fusion.8
  939.4 6.9 copy.127
  954.5 5.8 bitcast_add_fusion.8
  980.5 21.4 %all-to-all-done = bf16[2,360,768]{1,0,2:T(2,128)(2,1)S(1)} async-done(((bf16[2,360,768]{1,0,2:T(2,128)(2,1)}), bf16[2,360,768]{1,0,2:T(2,128)(2,1)S(1)}, u32[]{:S(2)}, u32[]{:S(2)}) %all-to-all-start) | async-done | bytes 1105952 | tf_op jit(solution)/shard_map/all_to_all | solution.py:132
  1004.1 6.4 fusion.30
  1012.5 32.5 %all_to_all.34 = bf16[8,720,96]{1,2,0:T(8,128)(2,1)S(1)} all-to-all(bf16[8,720,96]{1,2,0:T(8,128)(2,1)S(1)} %copy.82), channel_id=1, replica_groups=mesh['ord'=8,'blk'=4] {'ord'}, dimensions={0} | all-to-all | bytes 2211840 | tf_op jit(solution)/shard_map/all_to_all | solution.py:134
  (331 shorter events, 492.8 us)
Async XLA Ops:
  6.5 171.2 %all-gather.4.cloned.1.call-start = ((), (), s32[]{:S(2)}) async-start(), calls=%async_computation.2 | async-start | bytes 29491200 | tf_op jit(solution)/shard_map/all_gather | solution.py:124
  28.8 413.7 %all-gather.6.cloned.1.call-start = ((), (), s32[]{:S(2)}) async-start(), calls=%async_computation.3 | async-start | bytes 29491200 | tf_op jit(solution)/shard_map/all_gather | solution.py:124
  37.7 664.7 %all-gather.8.cloned.1.call-start = ((), (), s32[]{:S(2)}) async-start(), calls=%async_computation.4 | async-start | bytes 29491200 | tf_op jit(solution)/shard_map/all_gather | solution.py:124
  47.5 1.5 copy-start.6
  105.8 71.9 %copy-start.2 = (f32[16]{0:T(128)S(1)}, f32[16]{0:T(128)}, u32[]{:S(2)}) copy-start(f32[16]{0:T(128)} %param.13) | copy-start | bytes 196
  698.8 3.6 copy-start.3
  698.8 3.6 copy-start.4
  960.3 2.9 copy-start
  960.3 2.9 copy-start.1
  964.9 7.7 copy-start.5
  967.1 34.7 %all-to-all-start = ((bf16[2,360,768]{1,0,2:T(2,128)(2,1)}), bf16[2,360,768]{1,0,2:T(2,128)(2,1)S(1)}, u32[]{:S(2)}, u32[]{:S(2)}) async-start(bf16[2,360,768]{1,0,2:T(2,128)(2,1)} %copy.77), calls=%async_computation | async-start | bytes 2359296 | tf_op jit(solution)/shard_map/all_to_all | solution.py:132
Sparse Core Ops, SparseCore 0:
  28.9 148.7 all-gather.3
  179.3 146.0 all-gather.5
  327.0 146.0 all-gather.7
